TPU v7x, 32 devices: a whole 2x2x4 slice. The times are simulated.
32 devices in a mesh: py: 4 (over y, core), pz: 8 (over z, x).
Axes of the slice: x: 2, y: 2, z: 4, core: 2. Of those that a mesh axis runs over, the one named last changes fastest.
Arguments:
- wavefunctions: float32 [2, 8, 128, 128, 128], P(None, None, 'pz', 'py'), may hold values from -6 to 6
- potential: float32 [128, 128, 128], P('pz', 'py'), may hold values from -4 to 4
- cutoff_sq: int32 [1], replicated, may hold values from 2304 to 4096
- locked_mask: int32 [8], replicated, may hold values 0 or 1
Outputs:
- applied: float32 [2, 8, 128, 128, 128], P(None, None, 'pz', 'py')
- rayleigh: float32 [8], replicated
- residual_norm: float32 [8], replicated
All inputs are finite; a program needn't handle non-finite values.
Results may differ from a plain program's by a relative error of at most 0.00005.
Values sent between devices are 32-bit elements; how exact they have to be, the bound alone decides.
A program may use at most 64 MiB of HBM per device.

v0:
```python
import math
import jax
import jax.numpy as jnp
from jax import lax
from jax.sharding import PartitionSpec as P


def make_tables(length, inverse):
    counter = jnp.arange(length, dtype=jnp.int32)
    phase = counter[:, None] * counter[None, :] % length
    angle = 2.0 * math.pi / length * phase.astype(jnp.float32)
    if inverse:
        return (jnp.cos(angle) / length, jnp.sin(angle) / length)
    return (jnp.cos(angle), -jnp.sin(angle))


def transform_axis(field, axis, tables):
    cosines, sines = tables
    letters = "abcdefgh"[: field.ndim - 1]
    place = axis - 1
    source = letters[:place] + "n" + letters[place + 1 :]
    target = letters[:place] + "k" + letters[place + 1 :]
    form = source + ",kn->" + target
    real_part = field[0]
    imag_part = field[1]
    high = lax.Precision.HIGHEST
    out_real = jnp.einsum(form, real_part, cosines, precision=high) - jnp.einsum(
        form, imag_part, sines, precision=high
    )
    out_imag = jnp.einsum(form, real_part, sines, precision=high) + jnp.einsum(
        form, imag_part, cosines, precision=high
    )
    return jnp.stack([out_real, out_imag])


def signed_square(counter, length):
    signed = jnp.where(counter < length // 2, counter, counter - length)
    return signed * signed


def kinetic_table(first_sq, second_sq, third_sq, cutoff_sq, length):
    total = first_sq[:, None, None] + second_sq[None, :, None] + third_sq[None, None, :]
    keep = (total <= cutoff_sq[0]).astype(jnp.float32)
    return 0.5 * (math.pi / length) ** 2 * total.astype(jnp.float32) * keep


def slab_kinetic(field, cutoff_sq, forward, inverse):
    parts, bands, rows_z, rows_y, length = field.shape
    size_y = lax.axis_size("py")
    size_z = lax.axis_size("pz")
    along_x = transform_axis(field, 4, forward)
    flat = jnp.moveaxis(along_x, 1, 3).reshape(parts, rows_z, rows_y, bands * length)
    planes = lax.all_to_all(
        lax.all_to_all(flat, "py", split_axis=3, concat_axis=2, tiled=True),
        "pz",
        split_axis=3,
        concat_axis=1,
        tiled=True,
    )
    width = planes.shape[3]
    start = lax.axis_index("py") * (bands * length // size_y) + lax.axis_index("pz") * width
    column = start + jnp.arange(width, dtype=jnp.int32)
    full_counter = jnp.arange(length, dtype=jnp.int32)
    full_sq = signed_square(full_counter, length)
    kinetic = kinetic_table(
        full_sq, full_sq, signed_square(column % length, length), cutoff_sq, length
    )
    spectrum = transform_axis(transform_axis(planes, 1, forward), 2, forward) * kinetic
    spatial = transform_axis(transform_axis(spectrum, 2, inverse), 1, inverse)
    returned = lax.all_to_all(
        lax.all_to_all(spatial, "py", split_axis=2, concat_axis=3, tiled=True),
        "pz",
        split_axis=1,
        concat_axis=3,
        tiled=True,
    )
    ordered = returned.reshape(parts, rows_z, rows_y, size_z, size_y, width)
    ordered = jnp.swapaxes(ordered, 3, 4).reshape(parts, rows_z, rows_y, bands, length)
    return transform_axis(jnp.moveaxis(ordered, 3, 1), 4, inverse)


def apply_kinetic(field, cutoff_sq, forward, inverse):
    return slab_kinetic(field, cutoff_sq, forward, inverse)


def body(wavefunctions, potential, cutoff_sq, locked_mask):
    length = wavefunctions.shape[4]
    forward = make_tables(length, False)
    inverse = make_tables(length, True)
    blocks = wavefunctions.shape[1] // 4

    def one_block(block, result):
        piece = lax.dynamic_slice_in_dim(wavefunctions, block * 4, 4, 1)
        done = apply_kinetic(piece, cutoff_sq, forward, inverse)
        return lax.dynamic_update_slice_in_dim(result, done, block * 4, 1)

    kinetic_part = lax.fori_loop(0, blocks, one_block, jnp.zeros_like(wavefunctions))
    applied = kinetic_part + potential[None, None] * wavefunctions
    norm_local = jnp.sum(wavefunctions * wavefunctions, axis=(0, 2, 3, 4))
    correlation_local = jnp.sum(wavefunctions * applied, axis=(0, 2, 3, 4))
    norm_sq, correlation = lax.psum((norm_local, correlation_local), ("py", "pz"))
    rayleigh = correlation / norm_sq
    residual = applied - rayleigh[None, :, None, None, None] * wavefunctions
    residual_sq = lax.psum(jnp.sum(residual * residual, axis=(0, 2, 3, 4)), ("py", "pz"))
    residual_norm = jnp.sqrt(residual_sq / norm_sq) * (1.0 - locked_mask.astype(jnp.float32))
    return (applied, rayleigh, residual_norm)


def solution(mesh):
    in_specs = (P(None, None, "pz", "py", None), P("pz", "py", None), P(), P())
    out_specs = (P(None, None, "pz", "py", None), P(), P())
    return jax.shard_map(body, mesh=mesh, in_specs=in_specs, out_specs=out_specs, check_vma=False)
```

profile of v0, /device:TPU:0, one launch (start us, length us, event | category | flops | bytes accessed | tf_op | source)
XLA Modules:
  0.0 693.6 jit_solution(16688748125790381216)
XLA Ops:
  3.2 599.9 %while.18 = (s32[]{:T(128)}, f32[2,8,16,32,128]{4,3,2,1,0:T(8,128)}, f32[2,8,16,32,128]{4,3,2,1,0:T(8,128)}, s32[1]{0:T(128)}, s32[]{:T(128)}, /*index=5*/s32[]{...) while((s32[]{:T(128)}, ...), condition=%wide.region_1.2_spmd.clone.clone, body=%wide.region_0.1_spmd.clone.clone.sunk | while | flops 9676570624 | bytes 232916592 | solution.py:97
  13.3 7.5 %copy.142 = f32[2,16,32,4,128]{2,1,0,4,3:T(8,128)} copy(f32[2,16,32,4,128]{4,2,1,3,0:T(8,128)S(1)} %maximum_bitcast_fusion.2) | data formatting | bytes 4194304 | tf_op jit(solution)/shard_map/while/body/eval_jaxpr/reshape | solution.py:52
  26.9 30.2 %all_to_all.204 = f32[4,1,131072]{2,1,0:T(1,128)} all-to-all(f32[4,1,131072]{2,1,0:T(1,128)S(1)} %reshape.143), channel_id=1, replica_groups=mesh['py'=4,'pz'=8] {'py'}, dimensions={0} | all-to-all | bytes 4194304 | tf_op jit(solution)/shard_map/while/body/eval_jaxpr/all_to_all | solution.py:54
  57.6 7.7 %reduce.4 = f32[4,131072]{1,0:T(4,128)S(1)} reduce(f32[4,1,131072]{2,1,0:T(1,128)} %all_to_all.204, f32[]{:T(128)} %broadcast.656), dimensions={1}, to_apply=%all_to_all.178.reduce_sub_computation | reduce | bytes 4194308 | tf_op jit(solution)/shard_map/while/body/eval_jaxpr/all_to_all | solution.py:54
  81.3 6.9 all-to-all-start.1
  89.3 46.3 %all-to-all-done.1 = f32[2,16,128,128]{2,1,0,3:T(8,128)S(1)} async-done(((f32[2,16,128,128]{2,1,0,3:T(8,128)}), f32[2,16,128,128]{2,1,0,3:T(8,128)S(1)}, u32[]{:S(2)}, u32[]{:S(2)}) %all-to-all-start.1) | async-done | bytes 2097184 | tf_op jit(solution)/shard_map/while/body/eval_jaxpr/all_to_all | solution.py:53
  170.9 28.1 %all_to_all.205 = f32[2,128,128,16]{1,3,0,2:T(8,128)S(1)} all-to-all(f32[2,128,128,16]{1,3,0,2:T(8,128)S(1)} %copy.151), channel_id=1, replica_groups=mesh['py'=4,'pz'=8] {'py'}, dimensions={2} | all-to-all | bytes 4194304 | tf_op jit(solution)/shard_map/while/body/eval_jaxpr/all_to_all | solution.py:71
  203.8 7.2 %reshape.145 = f32[8,1,65536]{2,1,0:T(1,128)} reshape(f32[128,2,32,64]{3,2,1,0:T(8,128)} %bitcast.327) | data formatting | bytes 4194304 | tf_op jit(solution)/shard_map/while
  214.9 48.0 %all-to-all-done.3 = f32[8,1,65536]{2,1,0:T(1,128)S(1)} async-done(((f32[8,1,65536]{2,1,0:T(1,128)}), f32[8,1,65536]{2,1,0:T(1,128)S(1)}, u32[]{:S(2)}, u32[]{:S(2)}) %all-to-all-start.3) | async-done | bytes 2097184 | tf_op jit(solution)/shard_map/while/body/eval_jaxpr/all_to_all | solution.py:70
  264.8 7.2 %reduce.5 = f32[8,65536]{1,0:T(8,128)S(1)} reduce(f32[8,1,65536]{2,1,0:T(1,128)} %copy-done, f32[]{:T(128)} %broadcast.657), dimensions={1}, to_apply=%all_to_all.189.reduce_sub_computation | reduce | bytes 4194308 | tf_op jit(solution)/shard_map/while/body/eval_jaxpr/all_to_all | solution.py:70
  275.6 7.0 %copy.154 = f32[2,16,32,8,64]{2,4,3,1,0:T(8,128)} copy(f32[2,16,32,8,64]{4,2,0,1,3:T(8,128)} %bitcast.326) | data formatting | bytes 4194304 | tf_op jit(solution)/shard_map/while/body/eval_jaxpr/all_to_all | solution.py:70
  282.6 7.9 %copy.155 = f32[2,16,32,4,8,16]{2,5,4,3,1,0:T(8,128)} copy(f32[2,16,32,4,8,16]{2,5,3,4,1,0:T(8,128)} %bitcast.320) | data formatting | bytes 4194304 | tf_op jit(solution)/shard_map/while/body/eval_jaxpr/transpose | solution.py:78
  313.5 7.5 %copy.142 = f32[2,16,32,4,128]{2,1,0,4,3:T(8,128)} copy(f32[2,16,32,4,128]{4,2,1,3,0:T(8,128)S(1)} %maximum_bitcast_fusion.2) | data formatting | bytes 4194304 | tf_op jit(solution)/shard_map/while/body/eval_jaxpr/reshape | solution.py:52
  327.2 29.1 %all_to_all.204 = f32[4,1,131072]{2,1,0:T(1,128)} all-to-all(f32[4,1,131072]{2,1,0:T(1,128)S(1)} %reshape.143), channel_id=1, replica_groups=mesh['py'=4,'pz'=8] {'py'}, dimensions={0} | all-to-all | bytes 4194304 | tf_op jit(solution)/shard_map/while/body/eval_jaxpr/all_to_all | solution.py:54
  356.8 7.7 %reduce.4 = f32[4,131072]{1,0:T(4,128)S(1)} reduce(f32[4,1,131072]{2,1,0:T(1,128)} %all_to_all.204, f32[]{:T(128)} %broadcast.656), dimensions={1}, to_apply=%all_to_all.178.reduce_sub_computation | reduce | bytes 4194308 | tf_op jit(solution)/shard_map/while/body/eval_jaxpr/all_to_all | solution.py:54
  385.6 46.7 %all-to-all-done.1 = f32[2,16,128,128]{2,1,0,3:T(8,128)S(1)} async-done(((f32[2,16,128,128]{2,1,0,3:T(8,128)}), f32[2,16,128,128]{2,1,0,3:T(8,128)S(1)}, u32[]{:S(2)}, u32[]{:S(2)}) %all-to-all-start.1) | async-done | bytes 2097184 | tf_op jit(solution)/shard_map/while/body/eval_jaxpr/all_to_all | solution.py:53
  467.6 28.1 %all_to_all.205 = f32[2,128,128,16]{1,3,0,2:T(8,128)S(1)} all-to-all(f32[2,128,128,16]{1,3,0,2:T(8,128)S(1)} %copy.151), channel_id=1, replica_groups=mesh['py'=4,'pz'=8] {'py'}, dimensions={2} | all-to-all | bytes 4194304 | tf_op jit(solution)/shard_map/while/body/eval_jaxpr/all_to_all | solution.py:71
  500.5 7.2 %reshape.145 = f32[8,1,65536]{2,1,0:T(1,128)} reshape(f32[128,2,32,64]{3,2,1,0:T(8,128)} %bitcast.327) | data formatting | bytes 4194304 | tf_op jit(solution)/shard_map/while
  511.6 48.0 %all-to-all-done.3 = f32[8,1,65536]{2,1,0:T(1,128)S(1)} async-done(((f32[8,1,65536]{2,1,0:T(1,128)}), f32[8,1,65536]{2,1,0:T(1,128)S(1)}, u32[]{:S(2)}, u32[]{:S(2)}) %all-to-all-start.3) | async-done | bytes 2097184 | tf_op jit(solution)/shard_map/while/body/eval_jaxpr/all_to_all | solution.py:70
  561.5 7.2 %reduce.5 = f32[8,65536]{1,0:T(8,128)S(1)} reduce(f32[8,1,65536]{2,1,0:T(1,128)} %copy-done, f32[]{:T(128)} %broadcast.657), dimensions={1}, to_apply=%all_to_all.189.reduce_sub_computation | reduce | bytes 4194308 | tf_op jit(solution)/shard_map/while/body/eval_jaxpr/all_to_all | solution.py:70
  572.3 7.0 %copy.154 = f32[2,16,32,8,64]{2,4,3,1,0:T(8,128)} copy(f32[2,16,32,8,64]{4,2,0,1,3:T(8,128)} %bitcast.326) | data formatting | bytes 4194304 | tf_op jit(solution)/shard_map/while/body/eval_jaxpr/all_to_all | solution.py:70
  579.3 7.9 %copy.155 = f32[2,16,32,4,8,16]{2,5,4,3,1,0:T(8,128)} copy(f32[2,16,32,4,8,16]{2,5,3,4,1,0:T(8,128)} %bitcast.320) | data formatting | bytes 4194304 | tf_op jit(solution)/shard_map/while/body/eval_jaxpr/transpose | solution.py:78
  609.6 37.5 %all-reduce = (f32[8]{0:T(128)S(1)}, f32[8]{0:T(128)S(1)}) all-reduce(f32[8]{0:T(128)S(1)} %get-tuple-element.349, f32[8]{0:T(128)S(1)} %get-tuple-element.348), channel_id=1, replica_groups=mesh['py'=4,'pz'=8] {'py','pz'}, use_global_device_ids=true, to_apply=%region_3.4 | all-reduce | flops 16 | bytes 128 | tf_op jit(solution)/shard_map/psum | solution.py:101
  651.4 41.5 %psum.23 = f32[8]{0:T(128)S(1)} all-reduce(f32[8]{0:T(128)S(1)} %multiply_reduce_fusion), channel_id=1, replica_groups=mesh['py'=4,'pz'=8] {'py','pz'}, use_global_device_ids=true, to_apply=%region_7.8 | all-reduce | flops 8 | bytes 64 | tf_op jit(solution)/shard_map/psum | solution.py:104
  (130 shorter events, 209.5 us)
Async XLA Ops:
  3.2 599.9 %copy-start.4 = (f32[16,32,128]{2,1,0:T(8,128)S(1)}, f32[16,32,128]{2,1,0:T(8,128)}, u32[]{:S(2)}) copy-start(f32[16,32,128]{2,1,0:T(8,128)} %param.7) | copy-start | bytes 786436
  81.3 54.2 %all-to-all-start.1 = ((f32[2,16,128,128]{2,1,0,3:T(8,128)}), f32[2,16,128,128]{2,1,0,3:T(8,128)S(1)}, u32[]{:S(2)}, u32[]{:S(2)}) async-start(f32[2,16,128,128]{2,1,0,3:T(8,128)} %copy.145), calls=%async_computation.1 | async-start | bytes 4194304 | tf_op jit(solution)/shard_map/while/body/eval_jaxpr/all_to_all | solution.py:53
  138.5 3.5 copy-start.1
  211.0 51.9 %all-to-all-start.3 = ((f32[8,1,65536]{2,1,0:T(1,128)}), f32[8,1,65536]{2,1,0:T(1,128)S(1)}, u32[]{:S(2)}, u32[]{:S(2)}) async-start(f32[8,1,65536]{2,1,0:T(1,128)} %reshape.145), calls=%async_computation.3 | async-start | bytes 4194304 | tf_op jit(solution)/shard_map/while/body/eval_jaxpr/all_to_all | solution.py:70
  262.9 1.4 copy-start
  298.6 2.5 copy-start.2
  301.3 2.0 copy-start.3
  380.5 51.7 %all-to-all-start.1 = ((f32[2,16,128,128]{2,1,0,3:T(8,128)}), f32[2,16,128,128]{2,1,0,3:T(8,128)S(1)}, u32[]{:S(2)}, u32[]{:S(2)}) async-start(f32[2,16,128,128]{2,1,0,3:T(8,128)} %copy.145), calls=%async_computation.1 | async-start | bytes 4194304 | tf_op jit(solution)/shard_map/while/body/eval_jaxpr/all_to_all | solution.py:53
  435.2 3.5 copy-start.1
  507.7 51.9 %all-to-all-start.3 = ((f32[8,1,65536]{2,1,0:T(1,128)}), f32[8,1,65536]{2,1,0:T(1,128)S(1)}, u32[]{:S(2)}, u32[]{:S(2)}) async-start(f32[8,1,65536]{2,1,0:T(1,128)} %reshape.145), calls=%async_computation.3 | async-start | bytes 4194304 | tf_op jit(solution)/shard_map/while/body/eval_jaxpr/all_to_all | solution.py:70
  559.6 1.4 copy-start
  595.2 2.5 copy-start.2
  598.0 2.0 copy-start.3
  647.1 4.2 copy-start.5
  647.2 45.7 %copy-start.6 = (s32[8]{0:T(128)S(1)}, s32[8]{0:T(128)}, u32[]{:S(2)}) copy-start(s32[8]{0:T(128)} %param.9) | copy-start | bytes 100
where the time goes:
time: 697 us; the launch traced here: 694 us
  blocking collectives  195 us (28%)
  waiting for transfers between devices  189 us (27%)
  local copies, waits for them, and re-layouts  156 us (22%)
  matrix products  85.4 us (12%)
  other arithmetic  44.8 us (6%)
  starting transfers between devices  18.7 us (3%)
    all_to_all x2, waiting for transfers between devices, slab_kinetic(): lax.all_to_all(lax.all_to_all(spatial, 'py', split_axis=2, concat_axis=3,...  96 us
    all_to_all x2, waiting for transfers between devices, slab_kinetic(): lax.all_to_all(lax.all_to_all(flat, 'py', split_axis=3, concat_axis=2, ti...  92.9 us
    all_to_all x2, blocking collectives, slab_kinetic(): lax.all_to_all(flat, 'py', split_axis=3, concat_axis=2, tiled=True)  59.3 us
    all_to_all x2, blocking collectives, slab_kinetic(): lax.all_to_all(spatial, 'py', split_axis=2, concat_axis=3, tiled=True)  56.3 us
    while x24, local copies, waits for them, and re-layouts  52.9 us
    psum x1, blocking collectives, body(): lax.psum(jnp.sum(residual * residual, axis=(0, 2, 3, 4)), ('py', 'pz'))  41.5 us
    psum x1, blocking collectives, body(): lax.psum((norm_local, correlation_local), ('py', 'pz'))  37.5 us
    dot_general x12, matrix products, transform_axis(): jnp.einsum(form, imag_part, sines, precision=high)  22.5 us
  transfers between devices with their start and end apart: 4, of which 4 were waited for; matrix products, arithmetic and copies ran while one was open for 0% of the time, Pallas kernels for 0%

commit v1 on v0

--- a/solution.py
+++ b/solution.py
@@ -3,6 +3,22 @@
 import jax.numpy as jnp
 from jax import lax
 from jax.sharding import PartitionSpec as P
+
+
+def exchange_in_pairs(x, axis, split, join):
+    ways, here = (lax.axis_size(axis), lax.axis_index(axis))
+    width = x.shape[split] // ways
+    shape = list(x.shape)
+    shape[split] = width
+    height = shape[join]
+    shape[join] = height * ways
+    full = jnp.zeros(shape, x.dtype)
+    for mask in range(ways):
+        part = lax.dynamic_slice_in_dim(x, (here ^ mask) * width, width, axis=split)
+        if mask:
+            part = lax.ppermute(part, axis, [(d, d ^ mask) for d in range(ways)])
+        full = lax.dynamic_update_slice_in_dim(full, part, (here ^ mask) * height, axis=join)
+    return full
 
 
 def make_tables(length, inverse):
@@ -51,11 +67,7 @@
     along_x = transform_axis(field, 4, forward)
     flat = jnp.moveaxis(along_x, 1, 3).reshape(parts, rows_z, rows_y, bands * length)
     planes = lax.all_to_all(
-        lax.all_to_all(flat, "py", split_axis=3, concat_axis=2, tiled=True),
-        "pz",
-        split_axis=3,
-        concat_axis=1,
-        tiled=True,
+        exchange_in_pairs(flat, "py", 3, 2), "pz", split_axis=3, concat_axis=1, tiled=True
     )
     width = planes.shape[3]
     start = lax.axis_index("py") * (bands * length // size_y) + lax.axis_index("pz") * width

time: 697 us -> 877 us (1.26)
  local copies, waits for them, and re-layouts: 156 us -> 405 us
  blocking collectives: 195 us -> 136 us
  other arithmetic: 44.8 us -> 29.6 us
    dynamic_update_slice x0 -> x8, local copies, waits for them, and re-layouts: none -> 278 us  [exchange_in_pairs(): lax.dynamic_update_slice_in_dim(full, part, (here ^ mask) * height, axis=...]
    all_to_all x2 -> x0, blocking collectives: 59.3 us -> none  [slab_kinetic(): lax.all_to_all(flat, 'py', split_axis=3, concat_axis=2, tiled=True)]
    while x24 -> x28, local copies, waits for them, and re-layouts: 52.9 us -> 31 us
    all_to_all x10 -> x2, local copies, waits for them, and re-layouts: 23.3 us -> 2.43 us  [slab_kinetic(): lax.all_to_all(exchange_in_pairs(flat, 'py', 3, 2), 'pz', split_axis=3, c...]
    ppermute x0 -> x6, local copies, waits for them, and re-layouts: none -> 19.4 us  [exchange_in_pairs(): part = lax.ppermute(part, axis, [(d, d ^ mask) for d in range(ways)])]
    all_to_all x2 -> x0, other arithmetic: 15.4 us -> none  [slab_kinetic(): lax.all_to_all(flat, 'py', split_axis=3, concat_axis=2, tiled=True)]
    reshape x2 -> x0, local copies, waits for them, and re-layouts: 15 us -> none  [slab_kinetic(): jnp.moveaxis(along_x, 1, 3).reshape(parts, rows_z, rows_y, bands * length)]
  transfers between devices with their start and end apart: 4 -> 10, of which waited for: 4 -> 4; matrix products, arithmetic and copies ran while one was open for 0% -> 25% of each run, Pallas kernels for 0% -> 0%
where the time goes in v1:
time: 877 us; the launch traced here: 874 us
  local copies, waits for them, and re-layouts  405 us (46%)
  waiting for transfers between devices  190 us (22%)
  blocking collectives  136 us (16%)
  matrix products  85.2 us (10%)
  other arithmetic  29.6 us (3%)
  starting transfers between devices  23.4 us (3%)
    dynamic_update_slice x8, local copies, waits for them, and re-layouts, exchange_in_pairs(): lax.dynamic_update_slice_in_dim(full, part, (here ^ mask) * height, axis=...  278 us
    all_to_all x2, waiting for transfers between devices, slab_kinetic(): lax.all_to_all(lax.all_to_all(spatial, 'py', split_axis=2, concat_axis=3,...  96 us
    all_to_all x2, waiting for transfers between devices, slab_kinetic(): lax.all_to_all(exchange_in_pairs(flat, 'py', 3, 2), 'pz', split_axis=3, c...  94 us
    all_to_all x2, blocking collectives, slab_kinetic(): lax.all_to_all(spatial, 'py', split_axis=2, concat_axis=3, tiled=True)  56.7 us
    psum x1, blocking collectives, body(): lax.psum(jnp.sum(residual * residual, axis=(0, 2, 3, 4)), ('py', 'pz'))  41.5 us
    psum x1, blocking collectives, body(): lax.psum((norm_local, correlation_local), ('py', 'pz'))  37.5 us
    while x28, local copies, waits for them, and re-layouts  31 us
    dot_general x12, matrix products, transform_axis(): jnp.einsum(form, imag_part, sines, precision=high)  22.5 us
  transfers between devices with their start and end apart: 10, of which 4 were waited for; matrix products, arithmetic and copies ran while one was open for 25% of the time, Pallas kernels for 0%

profile of v1, /device:TPU:0, one launch (start us, length us, event | category | flops | bytes accessed | tf_op | source)
XLA Modules:
  0.0 873.9 jit_solution(9117618721708848060)
XLA Ops:
  3.2 780.1 %while.18 = (s32[]{:T(128)}, f32[2,8,16,32,128]{4,3,2,1,0:T(8,128)}, f32[2,8,16,32,128]{4,3,2,1,0:T(8,128)}, s32[1]{0:T(128)}, s32[]{:T(128)}, /*index=5*/s32[]{...) while((s32[]{:T(128)}, ...), condition=%wide.region_1.2_spmd.clone.clone, body=%wide.region_0.1_spmd.clone.clone.sunk | while | flops 9676570624 | bytes 237111504 | solution.py:109
  21.1 11.5 %dynamic_update_slice.72 = f32[2,16,128,128]{2,1,0,3:T(8,128)} dynamic-update-slice(f32[2,16,128,128]{2,1,0,3:T(8,128)} %broadcast.668, f32[2,16,32,128]{2,1,0,3:T(8,128)S(1)} %copy.149, s32[]{:T(128)} %constant.217.clone.1..sunk, s32[]{:T(128)} %constant.217.clone.1..sunk, s32[]{:T(128)S(6)} %select_n.419, s32[]{:T(128)} %constant.217.clone.1..sunk) | dynamic-update-slice | bytes 1048580 | tf_op jit(solution)/shard_map/while/body/eval_jaxpr/dynamic_update_slice | solution.py:20
  36.6 42.5 %dynamic_update_slice.73 = f32[2,16,128,128]{2,1,0,3:T(8,128)S(1)} dynamic-update-slice(f32[2,16,128,128]{2,1,0,3:T(8,128)S(1)} %copy-done.1, f32[2,16,32,128]{2,1,0,3:T(8,128)} %copy.150, s32[]{:T(128)} %constant.217.clone.1..sunk, s32[]{:T(128)} %constant.217.clone.1..sunk, s32[]{:T(128)S(6)} %select_n.420, s32[]{:T(128)} %constant.217.clone.1..sunk) | dynamic-update-slice | bytes 1048580 | tf_op jit(solution)/shard_map/while/body/eval_jaxpr/dynamic_update_slice | solution.py:20
  83.0 42.5 %dynamic_update_slice.74 = f32[2,16,128,128]{2,1,0,3:T(8,128)S(1)} dynamic-update-slice(f32[2,16,128,128]{2,1,0,3:T(8,128)S(1)} %dynamic_update_slice.73, f32[2,16,32,128]{2,1,0,3:T(8,128)} %copy.151, s32[]{:T(128)} %constant.217.clone.1..sunk, s32[]{:T(128)} %constant.217.clone.1..sunk, s32[]{:T(128)S(6)} %select_n.421, s32[]{:T(128)} %constant.217.clone.1..sunk) | dynamic-update-slice | bytes 1048580 | tf_op jit(solution)/shard_map/while/body/eval_jaxpr/dynamic_update_slice | solution.py:20
  128.7 42.4 %dynamic_update_slice.75 = f32[2,16,128,128]{2,1,0,3:T(8,128)} dynamic-update-slice(f32[2,16,128,128]{2,1,0,3:T(8,128)} %copy-done.2, f32[2,16,32,128]{2,1,0,3:T(8,128)S(1)} %copy.152, s32[]{:T(128)} %constant.217.clone.1..sunk, s32[]{:T(128)} %constant.217.clone.1..sunk, s32[]{:T(128)S(6)} %select_n.422, s32[]{:T(128)} %constant.217.clone.1..sunk) | dynamic-update-slice | bytes 1048580 | tf_op jit(solution)/shard_map/while/body/eval_jaxpr/dynamic_update_slice | solution.py:20
  178.7 46.8 %all-to-all-done = f32[2,16,128,128]{2,1,0,3:T(8,128)S(1)} async-done(((f32[2,16,128,128]{2,1,0,3:T(8,128)}), f32[2,16,128,128]{2,1,0,3:T(8,128)S(1)}, u32[]{:S(2)}, u32[]{:S(2)}) %all-to-all-start) | async-done | bytes 2097184 | tf_op jit(solution)/shard_map/while/body/eval_jaxpr/all_to_all | solution.py:69
  260.8 28.6 %all_to_all.148 = f32[2,128,128,16]{1,3,0,2:T(8,128)S(1)} all-to-all(f32[2,128,128,16]{1,3,0,2:T(8,128)S(1)} %copy.158), channel_id=1, replica_groups=mesh['py'=4,'pz'=8] {'py'}, dimensions={2} | all-to-all | bytes 4194304 | tf_op jit(solution)/shard_map/while/body/eval_jaxpr/all_to_all | solution.py:83
  294.2 7.2 reshape.139
  305.3 48.0 %all-to-all-done.2 = f32[8,1,65536]{2,1,0:T(1,128)S(1)} async-done(((f32[8,1,65536]{2,1,0:T(1,128)}), f32[8,1,65536]{2,1,0:T(1,128)S(1)}, u32[]{:S(2)}, u32[]{:S(2)}) %all-to-all-start.2) | async-done | bytes 2097184 | tf_op jit(solution)/shard_map/while/body/eval_jaxpr/all_to_all | solution.py:82
  355.1 7.2 reduce.2
  365.9 7.0 copy.161
  372.9 7.9 copy.162
  410.5 11.4 %dynamic_update_slice.72 = f32[2,16,128,128]{2,1,0,3:T(8,128)} dynamic-update-slice(f32[2,16,128,128]{2,1,0,3:T(8,128)} %broadcast.668, f32[2,16,32,128]{2,1,0,3:T(8,128)S(1)} %copy.149, s32[]{:T(128)} %constant.217.clone.1..sunk, s32[]{:T(128)} %constant.217.clone.1..sunk, s32[]{:T(128)S(6)} %select_n.419, s32[]{:T(128)} %constant.217.clone.1..sunk) | dynamic-update-slice | bytes 1048580 | tf_op jit(solution)/shard_map/while/body/eval_jaxpr/dynamic_update_slice | solution.py:20
  425.9 42.5 %dynamic_update_slice.73 = f32[2,16,128,128]{2,1,0,3:T(8,128)S(1)} dynamic-update-slice(f32[2,16,128,128]{2,1,0,3:T(8,128)S(1)} %copy-done.1, f32[2,16,32,128]{2,1,0,3:T(8,128)} %copy.150, s32[]{:T(128)} %constant.217.clone.1..sunk, s32[]{:T(128)} %constant.217.clone.1..sunk, s32[]{:T(128)S(6)} %select_n.420, s32[]{:T(128)} %constant.217.clone.1..sunk) | dynamic-update-slice | bytes 1048580 | tf_op jit(solution)/shard_map/while/body/eval_jaxpr/dynamic_update_slice | solution.py:20
  472.3 42.5 %dynamic_update_slice.74 = f32[2,16,128,128]{2,1,0,3:T(8,128)S(1)} dynamic-update-slice(f32[2,16,128,128]{2,1,0,3:T(8,128)S(1)} %dynamic_update_slice.73, f32[2,16,32,128]{2,1,0,3:T(8,128)} %copy.151, s32[]{:T(128)} %constant.217.clone.1..sunk, s32[]{:T(128)} %constant.217.clone.1..sunk, s32[]{:T(128)S(6)} %select_n.421, s32[]{:T(128)} %constant.217.clone.1..sunk) | dynamic-update-slice | bytes 1048580 | tf_op jit(solution)/shard_map/while/body/eval_jaxpr/dynamic_update_slice | solution.py:20
  517.9 42.4 %dynamic_update_slice.75 = f32[2,16,128,128]{2,1,0,3:T(8,128)} dynamic-update-slice(f32[2,16,128,128]{2,1,0,3:T(8,128)} %copy-done.2, f32[2,16,32,128]{2,1,0,3:T(8,128)S(1)} %copy.152, s32[]{:T(128)} %constant.217.clone.1..sunk, s32[]{:T(128)} %constant.217.clone.1..sunk, s32[]{:T(128)S(6)} %select_n.422, s32[]{:T(128)} %constant.217.clone.1..sunk) | dynamic-update-slice | bytes 1048580 | tf_op jit(solution)/shard_map/while/body/eval_jaxpr/dynamic_update_slice | solution.py:20
  565.4 47.2 %all-to-all-done = f32[2,16,128,128]{2,1,0,3:T(8,128)S(1)} async-done(((f32[2,16,128,128]{2,1,0,3:T(8,128)}), f32[2,16,128,128]{2,1,0,3:T(8,128)S(1)}, u32[]{:S(2)}, u32[]{:S(2)}) %all-to-all-start) | async-done | bytes 2097184 | tf_op jit(solution)/shard_map/while/body/eval_jaxpr/all_to_all | solution.py:69
  647.9 28.1 %all_to_all.148 = f32[2,128,128,16]{1,3,0,2:T(8,128)S(1)} all-to-all(f32[2,128,128,16]{1,3,0,2:T(8,128)S(1)} %copy.158), channel_id=1, replica_groups=mesh['py'=4,'pz'=8] {'py'}, dimensions={2} | all-to-all | bytes 4194304 | tf_op jit(solution)/shard_map/while/body/eval_jaxpr/all_to_all | solution.py:83
  680.7 7.2 reshape.139
  691.8 48.0 %all-to-all-done.2 = f32[8,1,65536]{2,1,0:T(1,128)S(1)} async-done(((f32[8,1,65536]{2,1,0:T(1,128)}), f32[8,1,65536]{2,1,0:T(1,128)S(1)}, u32[]{:S(2)}, u32[]{:S(2)}) %all-to-all-start.2) | async-done | bytes 2097184 | tf_op jit(solution)/shard_map/while/body/eval_jaxpr/all_to_all | solution.py:82
  741.7 7.2 reduce.2
  759.5 7.9 copy.162
  789.9 37.5 %all-reduce = (f32[8]{0:T(128)S(1)}, f32[8]{0:T(128)S(1)}) all-reduce(f32[8]{0:T(128)S(1)} %get-tuple-element.349, f32[8]{0:T(128)S(1)} %get-tuple-element.348), channel_id=1, replica_groups=mesh['py'=4,'pz'=8] {'py','pz'}, use_global_device_ids=true, to_apply=%region_3.4 | all-reduce | flops 16 | bytes 128 | tf_op jit(solution)/shard_map/psum | solution.py:113
  831.6 41.5 %psum.23 = f32[8]{0:T(128)S(1)} all-reduce(f32[8]{0:T(128)S(1)} %multiply_reduce_fusion), channel_id=1, replica_groups=mesh['py'=4,'pz'=8] {'py','pz'}, use_global_device_ids=true, to_apply=%region_7.8 | all-reduce | flops 8 | bytes 64 | tf_op jit(solution)/shard_map/psum | solution.py:116
  (152 shorter events, 213.9 us)
Async XLA Ops:
  3.2 780.1 %copy-start.6 = (f32[16,32,128]{2,1,0:T(8,128)S(1)}, f32[16,32,128]{2,1,0:T(8,128)}, u32[]{:S(2)}) copy-start(f32[16,32,128]{2,1,0:T(8,128)} %param.7) | copy-start | bytes 786436
  14.6 18.0 %collective-permute-start = (f32[2,16,32,128]{3,2,1,0:T(8,128)}, f32[2,16,32,128]{3,2,1,0:T(8,128)}, u32[]{:S(2)}, u32[]{:S(2)}) collective-permute-start(f32[2,16,32,128]{3,2,1,0:T(8,128)} %get-tuple-element.399), channel_id=1, source_target_pairs={{0,8},{8,0},{16,24},{24,16},{1,9},{9,1},{17,25},{25,17},{2,10},{10... | collective-permute-start | bytes 1572872 | tf_op jit(solution)/shard_map/while/body/eval_jaxpr/ppermute | solution.py:19
  15.1 64.0 %collective-permute-start.1 = (f32[2,16,32,128]{3,2,1,0:T(8,128)}, f32[2,16,32,128]{3,2,1,0:T(8,128)}, u32[]{:S(2)}, u32[]{:S(2)}) collective-permute-start(f32[2,16,32,128]{3,2,1,0:T(8,128)} %get-tuple-element.400), channel_id=1, source_target_pairs={{0,16},{8,24},{16,0},{24,8},{1,17},{9,25},{17,1},{25,9},{2,18},{10... | collective-permute-start | bytes 1572872 | tf_op jit(solution)/shard_map/while/body/eval_jaxpr/ppermute | solution.py:19
  17.6 109.2 %collective-permute-start.2 = (f32[2,16,32,128]{3,2,1,0:T(8,128)}, f32[2,16,32,128]{3,2,1,0:T(8,128)S(1)}, u32[]{:S(2)}, u32[]{:S(2)}) collective-permute-start(f32[2,16,32,128]{3,2,1,0:T(8,128)} %get-tuple-element.401), channel_id=1, source_target_pairs={{0,24},{8,16},{16,8},{24,0},{1,25},{9,17},{17,9},{25,1},{2,26},{10... | collective-permute-start | bytes 1572872 | tf_op jit(solution)/shard_map/while/body/eval_jaxpr/ppermute | solution.py:19
  32.6 4.0 copy-start.1
  125.5 1.3 copy-start.2
  171.1 54.4 %all-to-all-start = ((f32[2,16,128,128]{2,1,0,3:T(8,128)}), f32[2,16,128,128]{2,1,0,3:T(8,128)S(1)}, u32[]{:S(2)}, u32[]{:S(2)}) async-start(f32[2,16,128,128]{2,1,0,3:T(8,128)} %dynamic_update_slice.75), calls=%async_computation | async-start | bytes 4194304 | tf_op jit(solution)/shard_map/while/body/eval_jaxpr/all_to_all | solution.py:69
  228.5 3.4 copy-start.3
  301.4 51.9 %all-to-all-start.2 = ((f32[8,1,65536]{2,1,0:T(1,128)}), f32[8,1,65536]{2,1,0:T(1,128)S(1)}, u32[]{:S(2)}, u32[]{:S(2)}) async-start(f32[8,1,65536]{2,1,0:T(1,128)} %reshape.139), calls=%async_computation.2 | async-start | bytes 4194304 | tf_op jit(solution)/shard_map/while/body/eval_jaxpr/all_to_all | solution.py:82
  353.3 1.3 copy-start
  388.9 2.5 copy-start.4
  391.6 2.0 copy-start.5
  405.2 16.7 %collective-permute-start = (f32[2,16,32,128]{3,2,1,0:T(8,128)}, f32[2,16,32,128]{3,2,1,0:T(8,128)}, u32[]{:S(2)}, u32[]{:S(2)}) collective-permute-start(f32[2,16,32,128]{3,2,1,0:T(8,128)} %get-tuple-element.399), channel_id=1, source_target_pairs={{0,8},{8,0},{16,24},{24,16},{1,9},{9,1},{17,25},{25,17},{2,10},{10... | collective-permute-start | bytes 1572872 | tf_op jit(solution)/shard_map/while/body/eval_jaxpr/ppermute | solution.py:19
  405.2 63.2 %collective-permute-start.1 = (f32[2,16,32,128]{3,2,1,0:T(8,128)}, f32[2,16,32,128]{3,2,1,0:T(8,128)}, u32[]{:S(2)}, u32[]{:S(2)}) collective-permute-start(f32[2,16,32,128]{3,2,1,0:T(8,128)} %get-tuple-element.400), channel_id=1, source_target_pairs={{0,16},{8,24},{16,0},{24,8},{1,17},{9,25},{17,1},{25,9},{2,18},{10... | collective-permute-start | bytes 1572872 | tf_op jit(solution)/shard_map/while/body/eval_jaxpr/ppermute | solution.py:19
  406.1 110.0 %collective-permute-start.2 = (f32[2,16,32,128]{3,2,1,0:T(8,128)}, f32[2,16,32,128]{3,2,1,0:T(8,128)S(1)}, u32[]{:S(2)}, u32[]{:S(2)}) collective-permute-start(f32[2,16,32,128]{3,2,1,0:T(8,128)} %get-tuple-element.401), channel_id=1, source_target_pairs={{0,24},{8,16},{16,8},{24,0},{1,25},{9,17},{17,9},{25,1},{2,26},{10... | collective-permute-start | bytes 1572872 | tf_op jit(solution)/shard_map/while/body/eval_jaxpr/ppermute | solution.py:19
  421.9 4.0 copy-start.1
  514.7 1.3 copy-start.2
  560.3 52.2 %all-to-all-start = ((f32[2,16,128,128]{2,1,0,3:T(8,128)}), f32[2,16,128,128]{2,1,0,3:T(8,128)S(1)}, u32[]{:S(2)}, u32[]{:S(2)}) async-start(f32[2,16,128,128]{2,1,0,3:T(8,128)} %dynamic_update_slice.75), calls=%async_computation | async-start | bytes 4194304 | tf_op jit(solution)/shard_map/while/body/eval_jaxpr/all_to_all | solution.py:69
  615.5 3.4 copy-start.3
  687.9 51.9 %all-to-all-start.2 = ((f32[8,1,65536]{2,1,0:T(1,128)}), f32[8,1,65536]{2,1,0:T(1,128)S(1)}, u32[]{:S(2)}, u32[]{:S(2)}) async-start(f32[8,1,65536]{2,1,0:T(1,128)} %reshape.139), calls=%async_computation.2 | async-start | bytes 4194304 | tf_op jit(solution)/shard_map/while/body/eval_jaxpr/all_to_all | solution.py:82
  775.5 2.5 copy-start.4
  778.2 2.0 copy-start.5
  827.4 4.2 copy-start.7
  827.4 45.7 %copy-start.8 = (s32[8]{0:T(128)S(1)}, s32[8]{0:T(128)}, u32[]{:S(2)}) copy-start(s32[8]{0:T(128)} %param.9) | copy-start | bytes 100
  (1 other events, 1.3 us)
